TPU v7x, 32 devices: a whole 2x2x4 slice. The times are simulated.
32 devices in a mesh: dp: 4 (over z), ctx: 8 (over y, x, core).
Axes of the slice: x: 2, y: 2, z: 4, core: 2. Of those that a mesh axis runs over, the one named last changes fastest.
Arguments:
- item_ids: int32 [16, 2048], P('dp', 'ctx'), may hold values from 0 to 65535, as said below
- lengths: int32 [16], P('dp'), may hold values from 256 to 2048
- table: bfloat16 [65536, 512], P('dp'), may hold values from -6 to 6
- w_in: bfloat16 [512, 2048], replicated, may hold values from -0.25 to 0.25
- w_out: bfloat16 [512, 512], replicated, may hold values from -0.25 to 0.25
Outputs:
- layer_out: bfloat16 [16, 2048, 512], P('dp', 'ctx')
Inputs may be any that keep to these rules, and one draw needn't show every extreme that they name: `item_ids`: the owner of an id is id // 16384. In every user's block of 256 positions of one index of ctx, at most 128 ids have one owner; in each such block one owner, the same for all users at that index of ctx, has exactly 128.
All inputs are finite; a program needn't handle non-finite values.
Results may differ from a plain program's by a relative error of at most 0.0054.
Values may be sent and summed in bfloat16 or wider, within the bound.
A program may use at most 128 MiB of HBM per device.

v0:
```python
import functools
import math

import jax
import jax.numpy as jnp
from jax import lax
from jax.experimental import pallas as pl
from jax.experimental.pallas import tpu as pltpu
from jax.sharding import PartitionSpec as P

HEADS = 8
F32 = jnp.float32
BF16 = jnp.bfloat16
MESH = pl.DeviceIdType.MESH


def half_silu(h):
    return h + h * jnp.tanh(h)


def greet(axis, size, me, other):
    barrier = pltpu.get_barrier_semaphore()
    for step in range(1, size):
        peer = lax.rem(me + step, size)
        device = (peer, other) if axis == "dp" else (other, peer)
        pl.semaphore_signal(barrier, inc=1, device_id=device, device_id_type=MESH)


def index_kernel(owners, owned, cap, ids_ref, index_ref, slot_ref, ids_all, send_sem, recv_sem):
    users, _, rows = ids_ref.shape
    my_dp, my_ctx = lax.axis_index("dp"), lax.axis_index("ctx")
    greet("dp", owners, my_dp, my_ctx)
    pl.semaphore_wait(pltpu.get_barrier_semaphore(), owners - 1)
    copies = []
    for step in range(1, owners):
        copies.append(
            pltpu.make_async_remote_copy(
                src_ref=ids_ref,
                dst_ref=ids_all.at[my_dp],
                send_sem=send_sem.at[step],
                recv_sem=recv_sem.at[step],
                device_id=(lax.rem(my_dp + step, owners), my_ctx),
                device_id_type=MESH,
            )
        )
        copies[-1].start()
    earlier = lax.broadcasted_iota(jnp.int32, (rows, rows), 0)
    later = lax.broadcasted_iota(jnp.int32, (rows, rows), 1)
    upto = (earlier <= later).astype(BF16)
    own = ids_ref[...].reshape(users, rows)
    masks = jnp.concatenate(
        [((own >= o * owned) & (own < (o + 1) * owned)).astype(F32) for o in range(owners)], axis=0
    )
    ranks = jnp.dot(masks.astype(BF16), upto, preferred_element_type=F32) - 1.0
    slots = jnp.zeros((users, rows), F32)
    for o in range(owners):
        part = slice(o * users, (o + 1) * users)
        slots = slots + masks[part] * (ranks[part] + float(o * cap))
    slot_ref[...] = slots.astype(jnp.int32).reshape(users, 1, rows)
    ids_all[my_dp] = ids_ref[...]
    for copy in copies:
        copy.wait()
    wanted = ids_all[...].reshape(owners * users, rows) - my_dp * owned
    mine = ((wanted >= 0) & (wanted < owned)).astype(F32)
    rank = jnp.dot(mine.astype(BF16), upto, preferred_element_type=F32)
    rank = jnp.where(mine > 0.0, rank - 1.0, -1.0).astype(jnp.int32)
    digits = [wanted & 255, (wanted >> 8) & 255, (wanted >> 16) & 255]
    slot_iota = lax.broadcasted_iota(jnp.int32, (cap, rows), 0)
    lines = []
    for n in range(owners * users):
        hot = (rank[n : n + 1] == slot_iota).astype(BF16)
        digit = jnp.concatenate([d[n : n + 1] for d in digits] + [jnp.zeros((5, rows), jnp.int32)], axis=0)
        found = lax.dot_general(
            digit.astype(F32).astype(BF16), hot, (((1,), (1,)), ((), ())), preferred_element_type=F32
        )
        lines.append(found[0:1] + 256.0 * found[1:2] + 65536.0 * found[2:3])
    index_ref[...] = jnp.concatenate(lines, axis=0).astype(jnp.int32)


def layer_kernel(
    owners, group, lengths_ref, picked_ref, slot_ref, w_in_ref, w_out_ref, out_ref,
    rows_all, w_in_t, embedded_all, gate_all, send_all, recv_all, ret_all, attn_all,
    q_nat, v_nat, k_lane,
    z_send, z_recv, c_send, c_recv, r_send, r_recv,
):
    _, users, cap, width = picked_ref.shape
    rows = slot_ref.shape[2]
    size = width // HEADS
    per_round = group // HEADS
    rounds = users // per_round
    my_dp, my_ctx = lax.axis_index("dp"), lax.axis_index("ctx")
    my_user, my_head = my_ctx // HEADS, lax.rem(my_ctx, HEADS)
    greet("dp", owners, my_dp, my_ctx)
    greet("ctx", group, my_ctx, my_dp)
    pl.semaphore_wait(pltpu.get_barrier_semaphore(), owners + group - 2)

    def row_copy(u, step):
        peer = lax.rem(my_dp + step, owners)
        return pltpu.make_async_remote_copy(
            src_ref=picked_ref.at[peer, u],
            dst_ref=rows_all.at[u, my_dp],
            send_sem=z_send.at[u, step],
            recv_sem=z_recv.at[u, step],
            device_id=(peer, my_ctx),
            device_id_type=MESH,
        )

    def unit_copy(r, step):
        peer = lax.rem(my_ctx + step, group)
        return pltpu.make_async_remote_copy(
            src_ref=send_all.at[r * per_round + peer // HEADS, lax.rem(peer, HEADS)],
            dst_ref=recv_all.at[r, my_ctx],
            send_sem=c_send.at[r, step],
            recv_sem=c_recv.at[r, step],
            device_id=(my_dp, peer),
            device_id_type=MESH,
        )

    def back_copy(r, step):
        peer = lax.rem(my_ctx + step, group)
        return pltpu.make_async_remote_copy(
            src_ref=ret_all.at[r, peer],
            dst_ref=attn_all.at[r * per_round + my_user, my_head],
            send_sem=r_send.at[r, step],
            recv_sem=r_recv.at[r, step],
            device_id=(my_dp, peer),
            device_id_type=MESH,
        )

    for u in range(users):
        for step in range(1, owners):
            row_copy(u, step).start()
    for u in range(users):
        rows_all[u, my_dp] = picked_ref[my_dp, u]
    for part in range(4):
        cols = slice(part * width, (part + 1) * width)
        w_in_t[cols, :] = w_in_ref[:, cols].T

    def project(u):
        for step in range(1, owners):
            row_copy(u, step).wait_recv()
        found = rows_all[u].reshape(owners * cap, width)
        slot_iota = lax.broadcasted_iota(jnp.int32, (owners * cap, rows), 0)
        hot = (slot_ref[u] == slot_iota).astype(BF16)
        embedded = lax.dot_general(hot, found, (((0,), (0,)), ((), ())), preferred_element_type=F32)
        embedded_all[u] = embedded.astype(BF16)
        center = embedded - jnp.mean(embedded, axis=-1, keepdims=True)
        spread = jnp.mean(center * center, axis=-1, keepdims=True)
        normed = (center * lax.rsqrt(spread + 1e-05)).astype(BF16)

        def part_of(part):
            half = 0.5 * lax.dot_general(
                w_in_t[part * width : (part + 1) * width, :],
                normed,
                (((1,), (1,)), ((), ())),
                preferred_element_type=F32,
            )
            return half_silu(half).astype(BF16)

        scale = 0.5 / math.sqrt(size)
        query = (part_of(2).astype(F32) * scale).astype(BF16)
        send_all[u, :, 0:size, :] = query.reshape(HEADS, size, rows)
        send_all[u, :, size : 2 * size, :] = part_of(3).reshape(HEADS, size, rows)
        send_all[u, :, 2 * size : 3 * size, :] = part_of(1).reshape(HEADS, size, rows)
        gate_all[u] = part_of(0)

    def attend(r):
        length = lengths_ref[r * per_round + my_user]
        for j in range(group):
            block = slice(j * rows, (j + 1) * rows)
            q_nat[block, :] = recv_all[r, j, 0:size, :].T
            k_lane[:, block] = recv_all[r, j, size : 2 * size, :]
            position = j * rows + lax.broadcasted_iota(jnp.int32, (size, rows), 1)
            value = recv_all[r, j, 2 * size : 3 * size, :].astype(F32)
            v_nat[block, :] = jnp.where(position < length, value, 0.0).T.astype(BF16)
        query_pos = lax.broadcasted_iota(jnp.int32, (rows, rows), 0)
        key_pos = lax.broadcasted_iota(jnp.int32, (rows, rows), 1)
        for i in range(group):
            query = q_nat[i * rows : (i + 1) * rows, :]
            total = jnp.zeros((rows, size), F32)
            for j in range(i + 1):
                block = slice(j * rows, (j + 1) * rows)
                half = jnp.dot(query, k_lane[:, block], preferred_element_type=F32)
                weight = half_silu(half)
                if j == i:
                    weight = jnp.where(key_pos <= query_pos, weight, 0.0)
                total = total + jnp.dot(weight.astype(BF16), v_nat[block, :], preferred_element_type=F32)
            ret_all[r, i] = total.T.astype(BF16)

    def finish(u):
        attended = attn_all[u].reshape(width, rows).astype(F32)
        center = attended - jnp.mean(attended, axis=0, keepdims=True)
        spread = jnp.mean(center * center, axis=0, keepdims=True)
        gated = (center * lax.rsqrt(spread + 1e-05) * gate_all[u].astype(F32)).astype(BF16)
        mixed = lax.dot_general(gated, w_out_ref[...], (((0,), (0,)), ((), ())), preferred_element_type=F32)
        out_ref[u] = (embedded_all[u].astype(F32) + mixed).astype(BF16)

    def step_body(t, carry):
        @pl.when(t < rounds)
        def _():
            for k in range(per_round):
                project(t * per_round + k)
            for step in range(1, group):
                unit_copy(t, step).start()
            recv_all[t, my_ctx] = send_all[t * per_round + my_user, my_head]

        @pl.when((t >= 1) & (t <= rounds))
        def _():
            r = t - 1
            for step in range(1, group):
                unit_copy(r, step).wait_recv()
            attend(r)
            for step in range(1, group):
                back_copy(r, step).start()
            attn_all[r * per_round + my_user, my_head] = ret_all[r, my_ctx]

        @pl.when(t >= 2)
        def _():
            r = t - 2
            for step in range(1, group):
                back_copy(r, step).wait_recv()
            for k in range(per_round):
                finish(r * per_round + k)

        return carry

    lax.fori_loop(0, rounds + 2, step_body, 0)
    for u in range(users):
        for step in range(1, owners):
            row_copy(u, step).wait_send()
    for r in range(rounds):
        for step in range(1, group):
            unit_copy(r, step).wait_send()
            back_copy(r, step).wait_send()


def per_device(item_ids, lengths, table, w_in, w_out):
    users, rows = item_ids.shape
    owned, width = table.shape
    owners, group = lax.axis_size("dp"), lax.axis_size("ctx")
    cap = 2 * rows // owners
    size = width // HEADS
    per_round = group // HEADS
    rounds = users // per_round
    vmem = pl.BlockSpec(memory_space=pltpu.VMEM)
    index, slots = pl.pallas_call(
        functools.partial(index_kernel, owners, owned, cap),
        out_shape=(
            jax.ShapeDtypeStruct((owners * users, cap), jnp.int32),
            jax.ShapeDtypeStruct((users, 1, rows), jnp.int32),
        ),
        in_specs=[vmem],
        out_specs=(vmem, vmem),
        scratch_shapes=[
            pltpu.VMEM((owners, users, 1, rows), jnp.int32),
            pltpu.SemaphoreType.DMA((owners,)),
            pltpu.SemaphoreType.DMA((owners,)),
        ],
        compiler_params=pltpu.CompilerParams(collective_id=0, has_side_effects=True),
    )(item_ids.reshape(users, 1, rows))
    picked = jnp.take(table, index.reshape(-1), axis=0, mode="clip").reshape(owners, users, cap, width)
    return pl.pallas_call(
        functools.partial(layer_kernel, owners, group),
        out_shape=jax.ShapeDtypeStruct((users, rows, width), BF16),
        in_specs=[pl.BlockSpec(memory_space=pltpu.SMEM), vmem, vmem, vmem, vmem],
        out_specs=vmem,
        scratch_shapes=[
            pltpu.VMEM((users, owners, cap, width), BF16),
            pltpu.VMEM((4 * width, width), BF16),
            pltpu.VMEM((users, rows, width), BF16),
            pltpu.VMEM((users, width, rows), BF16),
            pltpu.VMEM((users, HEADS, 3 * size, rows), BF16),
            pltpu.VMEM((rounds, group, 3 * size, rows), BF16),
            pltpu.VMEM((rounds, group, size, rows), BF16),
            pltpu.VMEM((users, HEADS, size, rows), BF16),
            pltpu.VMEM((group * rows, size), BF16),
            pltpu.VMEM((group * rows, size), BF16),
            pltpu.VMEM((size, group * rows), BF16),
            pltpu.SemaphoreType.DMA((users, owners)),
            pltpu.SemaphoreType.DMA((users, owners)),
            pltpu.SemaphoreType.DMA((rounds, group)),
            pltpu.SemaphoreType.DMA((rounds, group)),
            pltpu.SemaphoreType.DMA((rounds, group)),
            pltpu.SemaphoreType.DMA((rounds, group)),
        ],
        compiler_params=pltpu.CompilerParams(
            collective_id=1, has_side_effects=True, vmem_limit_bytes=56 * 1024 * 1024
        ),
    )(lengths, picked, slots, w_in, w_out)


def solution(mesh):
    return jax.shard_map(
        per_device,
        mesh=mesh,
        in_specs=(P("dp", "ctx"), P("dp"), P("dp", None), P(), P()),
        out_specs=P("dp", "ctx", None),
        check_vma=False,
    )
```

profile of v0, /device:TPU:15, one launch (start us, length us, event | category | flops | bytes accessed | tf_op | source)
XLA Modules:
  0.0 114.7 jit_solution(16902219375514810601)
XLA Ops:
  0.0 1.3 %reshape.8.ids_ref = s32[4,1,256]{2,1,0:T(1,128)} reshape(s32[4,256]{1,0:T(4,128)} %param.5) | data formatting | bytes 8192 | tf_op jit(solution)/shard_map/reshape | solution.py:260
  1.3 6.7 %shard_map.55 = (s32[16,128]{1,0:T(8,128)}, s32[4,1,256]{2,1,0:T(1,128)}) custom-call(s32[4,1,256]{2,1,0:T(1,128)} %reshape.8.ids_ref), custom_call_target="tpu_custom_call" | custom-call | tf_op jit(solution)/shard_map/pallas_call | solution.py:246
  8.0 0.7 bitcast_clamp_fusion
  8.7 17.2 %gather_fusion = bf16[2048,512]{1,0:T(8,128)(2,1)} fusion(bf16[16384,512]{1,0:T(8,128)(2,1)} %param.7, s32[2048]{0:T(1024)S(1)} %bitcast_clamp_fusion), kind=kCustom, calls=%fused_computation | custom fusion | bytes 4202496 | tf_op jit(solution)/shard_map/jit(_take)/gather | solution.py:261
  25.8 86.6 %shard_map.56 = bf16[4,256,512]{2,1,0:T(8,128)(2,1)} custom-call(s32[4]{0:T(128)} %lengths_ref.1, bf16[4,4,128,512]{3,2,1,0:T(8,128)(2,1)} %bitcast.3, s32[4,1,256]{2,1,0:T(1,128)} %get-tuple-element.8.slot_ref, bf16[512,2048]{1,0:T(8,128)(2,1)} %w_in_ref.1, bf16[512,512]{1,0:T(8,128)(2,1)} %w_out_ref.1), custom_call_target="tpu_custom_call" | custom-call | tf_op jit(solution)/shard_map/pallas_call | solution.py:262
  112.5 2.3 %copy.7 = bf16[4,256,512]{2,1,0:T(8,128)(2,1)} copy(bf16[4,256,512]{2,1,0:T(8,128)(2,1)} %shard_map.56) | data formatting | bytes 2097152
where the time goes:
time: 116 us; the launch traced here: 115 us
  Pallas kernels  93.3 us (80%)
  local copies, waits for them, and re-layouts  20.7 us (18%)
    pallas_call x1, Pallas kernels, per_device(): pl.pallas_call(functools.partial(layer_kernel, owners, group), out_shape=...  86.6 us
    gather x1, local copies, waits for them, and re-layouts, per_device(): jnp.take(table, index.reshape(-1), axis=0, mode='clip')  17.2 us
    pallas_call x1, Pallas kernels, per_device(): pl.pallas_call(functools.partial(index_kernel, owners, owned, cap), out_s...  6.68 us

commit v1 on v0

v1 whole, which is shorter than its diff:
```python
import functools
import math

import jax
import jax.numpy as jnp
from jax import lax
from jax.experimental import pallas as pl
from jax.experimental.pallas import tpu as pltpu
from jax.sharding import PartitionSpec as P

HEADS = 8
F32 = jnp.float32
BF16 = jnp.bfloat16
MESH = pl.DeviceIdType.MESH


def half_silu(h):
    return h + h * jnp.tanh(h)


def greet(axis, size, me, other):
    barrier = pltpu.get_barrier_semaphore()
    for step in range(1, size):
        peer = lax.rem(me + step, size)
        device = (peer, other) if axis == "dp" else (other, peer)
        pl.semaphore_signal(barrier, inc=1, device_id=device, device_id_type=MESH)


def layer_kernel(
    owners, group, lengths_ref, ids_ref, table_ref, w_in_ref, w_out_ref, out_ref,
    ids_all, slot_all, index_vmem, index_smem, table_chunk, table_wide, row_wide, picked,
    w_in_all, w_out_all, rows_all, w_in_t, embedded_all, gate_all, send_all, recv_all,
    ret_all, attn_all, q_nat, v_nat, k_lane,
    t_sem, w_sem, i_sem, n_send, n_recv, z_send, z_recv, c_send, c_recv, r_send, r_recv,
):
    owned, width = table_ref.shape
    users, rows = ids_ref.shape
    cap = row_wide.shape[0]
    size = width // HEADS
    per_round = group // HEADS
    rounds = users // per_round
    depth, chunk = table_chunk.shape[:2]
    chunks = owned // chunk
    my_dp, my_ctx = lax.axis_index("dp"), lax.axis_index("ctx")
    my_user, my_head = my_ctx // HEADS, lax.rem(my_ctx, HEADS)

    def table_copy(c):
        return pltpu.make_async_copy(
            table_ref.at[pl.ds(pl.multiple_of(c * chunk, chunk), chunk), :],
            table_chunk.at[lax.rem(c, depth)],
            t_sem.at[lax.rem(c, depth)],
        )

    for c in range(depth):
        table_copy(c).start()
    greet("dp", owners, my_dp, my_ctx)
    greet("ctx", group, my_ctx, my_dp)
    pl.semaphore_wait(pltpu.get_barrier_semaphore(), owners + group - 2)

    def id_copy(step):
        return pltpu.make_async_remote_copy(
            src_ref=ids_ref,
            dst_ref=ids_all.at[my_dp],
            send_sem=n_send.at[step],
            recv_sem=n_recv.at[step],
            device_id=(lax.rem(my_dp + step, owners), my_ctx),
            device_id_type=MESH,
        )

    for step in range(1, owners):
        id_copy(step).start()

    def widen(c, carry):
        table_copy(c).wait()
        table_wide[pl.ds(pl.multiple_of(c * chunk, chunk), chunk), :] = table_chunk[lax.rem(c, depth)].astype(F32)

        @pl.when(c + depth < chunks)
        def _():
            table_copy(c + depth).start()

        return carry

    lax.fori_loop(0, chunks, widen, 0)
    w_in_copy = pltpu.make_async_copy(w_in_ref, w_in_all, w_sem.at[0])
    w_out_copy = pltpu.make_async_copy(w_out_ref, w_out_all, w_sem.at[1])
    w_in_copy.start()
    w_out_copy.start()

    earlier = lax.broadcasted_iota(jnp.int32, (rows, rows), 0)
    later = lax.broadcasted_iota(jnp.int32, (rows, rows), 1)
    upto = (earlier <= later).astype(BF16)
    own = ids_ref[...]
    ids_all[my_dp] = own
    for step in range(1, owners):
        id_copy(step).wait_recv()
    wanted = jnp.concatenate([ids_all[o] for o in range(owners)], axis=0) - my_dp * owned
    mine = ((wanted >= 0) & (wanted < owned)).astype(F32)
    rank = jnp.dot(mine.astype(BF16), upto, preferred_element_type=F32)
    rank = jnp.where(mine > 0.0, rank - 1.0, -1.0).astype(jnp.int32)
    digits = [wanted & 255, (wanted >> 8) & 255, (wanted >> 16) & 255]
    slot_iota = lax.broadcasted_iota(jnp.int32, (cap, rows), 0)
    lines = []
    for n in range(owners * users):
        hot = (rank[n : n + 1] == slot_iota).astype(BF16)
        digit = jnp.concatenate([d[n : n + 1] for d in digits] + [jnp.zeros((5, rows), jnp.int32)], axis=0)
        found = lax.dot_general(
            digit.astype(F32).astype(BF16), hot, (((1,), (1,)), ((), ())), preferred_element_type=F32
        )
        lines.append(found[0:1] + 256.0 * found[1:2] + 65536.0 * found[2:3])
    index_vmem[...] = jnp.concatenate(lines, axis=0).astype(jnp.int32)
    index_copy = pltpu.make_async_copy(index_vmem, index_smem, i_sem)
    index_copy.start()
    masks = jnp.concatenate(
        [((own >= o * owned) & (own < (o + 1) * owned)).astype(F32) for o in range(owners)], axis=0
    )
    ranks = jnp.dot(masks.astype(BF16), upto, preferred_element_type=F32) - 1.0
    slots = jnp.zeros((users, rows), F32)
    for o in range(owners):
        part = slice(o * users, (o + 1) * users)
        slots = slots + masks[part] * (ranks[part] + float(o * cap))
    slots = slots.astype(jnp.int32)
    for u in range(users):
        slot_all[u] = slots[u : u + 1]
    index_copy.wait()

    def row_copy(u, step):
        peer = lax.rem(my_dp + step, owners)
        return pltpu.make_async_remote_copy(
            src_ref=picked.at[u, step],
            dst_ref=rows_all.at[u, my_dp],
            send_sem=z_send.at[u, step],
            recv_sem=z_recv.at[u, step],
            device_id=(peer, my_ctx),
            device_id_type=MESH,
        )

    def pick(u, step):
        line = lax.rem(my_dp + step, owners) * users + u
        batch = 16

        def pick_batch(k, carry):
            base = pl.multiple_of(k * batch, batch)
            for n in range(batch):
                row = jnp.clip(index_smem[line, base + n], 0, owned - 1)
                row_wide[pl.ds(base + n, 1), :] = table_wide[pl.ds(row, 1), :]
            return carry

        lax.fori_loop(0, cap // batch, pick_batch, 0)
        return row_wide[...].astype(BF16)

    def pick_user(u, carry):
        for step in range(1, owners):
            picked[u, step] = pick(u, step)
            row_copy(u, step).start()
        rows_all[u, my_dp] = pick(u, 0)
        return carry

    lax.fori_loop(0, users, pick_user, 0)
    w_in_copy.wait()
    w_out_copy.wait()
    for part in range(4):
        cols = slice(part * width, (part + 1) * width)
        w_in_t[cols, :] = w_in_all[:, cols].T

    def unit_copy(r, step):
        peer = lax.rem(my_ctx + step, group)
        return pltpu.make_async_remote_copy(
            src_ref=send_all.at[r * per_round + peer // HEADS, lax.rem(peer, HEADS)],
            dst_ref=recv_all.at[r, my_ctx],
            send_sem=c_send.at[r, step],
            recv_sem=c_recv.at[r, step],
            device_id=(my_dp, peer),
            device_id_type=MESH,
        )

    def back_copy(r, peer, sender):
        return pltpu.make_async_remote_copy(
            src_ref=ret_all.at[r, peer],
            dst_ref=attn_all.at[r * per_round + my_user, my_head],
            send_sem=r_send.at[r, peer],
            recv_sem=r_recv.at[r, sender],
            device_id=(my_dp, peer),
            device_id_type=MESH,
        )

    def part_of(part, normed):
        half = 0.5 * lax.dot_general(
            w_in_t[part * width : (part + 1) * width, :],
            normed,
            (((1,), (1,)), ((), ())),
            preferred_element_type=F32,
        )
        return half_silu(half).astype(BF16)

    def project(u):
        for step in range(1, owners):
            row_copy(u, step).wait_recv()
        found = rows_all[u].reshape(owners * cap, width)
        slot_iota = lax.broadcasted_iota(jnp.int32, (owners * cap, rows), 0)
        hot = (slot_all[u] == slot_iota).astype(BF16)
        embedded = lax.dot_general(hot, found, (((0,), (0,)), ((), ())), preferred_element_type=F32)
        embedded_all[u] = embedded.astype(BF16)
        center = embedded - jnp.mean(embedded, axis=-1, keepdims=True)
        spread = jnp.mean(center * center, axis=-1, keepdims=True)
        normed = (center * lax.rsqrt(spread + 1e-05)).astype(BF16)

        scale = 0.5 / math.sqrt(size)
        query = (part_of(2, normed).astype(F32) * scale).astype(BF16)
        send_all[u, :, 0:size, :] = query.reshape(HEADS, size, rows)
        send_all[u, :, size : 2 * size, :] = part_of(3, normed).reshape(HEADS, size, rows)
        send_all[u, :, 2 * size : 3 * size, :] = part_of(1, normed).reshape(HEADS, size, rows)
        return normed

    def attend(r):
        length = lengths_ref[r * per_round + my_user]
        for j in range(group):
            block = slice(j * rows, (j + 1) * rows)
            q_nat[block, :] = recv_all[r, j, 0:size, :].T
            k_lane[:, block] = recv_all[r, j, size : 2 * size, :]
            position = j * rows + lax.broadcasted_iota(jnp.int32, (size, rows), 1)
            value = recv_all[r, j, 2 * size : 3 * size, :].astype(F32)
            v_nat[block, :] = jnp.where(position < length, value, 0.0).T.astype(BF16)
        query_pos = lax.broadcasted_iota(jnp.int32, (rows, rows), 0)
        key_pos = lax.broadcasted_iota(jnp.int32, (rows, rows), 1)
        extra_row = lax.broadcasted_iota(jnp.int32, (ret_all.shape[2] - size, rows), 0)
        for i in range(group):
            query = q_nat[i * rows : (i + 1) * rows, :]
            total = jnp.zeros((rows, size), F32)
            for j in range(i + 1):
                block = slice(j * rows, (j + 1) * rows)
                half = jnp.dot(query, k_lane[:, block], preferred_element_type=F32)
                weight = half_silu(half)
                if j == i:
                    weight = jnp.where(key_pos <= query_pos, weight, 0.0)
                total = total + jnp.dot(weight.astype(BF16), v_nat[block, :], preferred_element_type=F32)
            total = total.T
            middle = jnp.mean(total, axis=0, keepdims=True)
            high = middle.astype(BF16).astype(F32)
            low = (middle - high).astype(BF16).astype(F32)
            extra = jnp.where(extra_row == 0, high, jnp.where(extra_row == 1, low, 0.0))
            extra = jnp.where(extra_row == 2, middle - high - low, extra)
            ret_all[r, i, 0:size, :] = (total - middle).astype(BF16)
            ret_all[r, i, size:, :] = extra.astype(BF16)

            @pl.when(my_ctx != i)
            def _():
                back_copy(r, i, my_ctx).start()


    def finish(u):
        middle = jnp.sum(attn_all[u, :, size:, :].astype(F32), axis=1, keepdims=True)
        middle = middle - jnp.mean(middle, axis=0, keepdims=True)
        attended = (attn_all[u, :, 0:size, :].astype(F32) + middle).reshape(width, rows)
        center = attended - jnp.mean(attended, axis=0, keepdims=True)
        spread = jnp.mean(center * center, axis=0, keepdims=True)
        gated = (center * lax.rsqrt(spread + 1e-05) * gate_all[u].astype(F32)).astype(BF16)
        mixed = lax.dot_general(gated, w_out_all[...], (((0,), (0,)), ((), ())), preferred_element_type=F32)
        out_ref[u] = (embedded_all[u].astype(F32) + mixed).astype(BF16)

    def step_body(t, carry):
        @pl.when(t < rounds)
        def _():
            normed = [project(t * per_round + k) for k in range(per_round)]
            for step in range(1, group):
                unit_copy(t, step).start()
            for k in range(per_round):
                gate_all[t * per_round + k] = part_of(0, normed[k])
            recv_all[t, my_ctx] = send_all[t * per_round + my_user, my_head]

        @pl.when((t >= 1) & (t <= rounds))
        def _():
            r = t - 1
            for step in range(1, group):
                unit_copy(r, step).wait_recv()
            attend(r)
            attn_all[r * per_round + my_user, my_head] = ret_all[r, my_ctx]

        @pl.when(t >= 2)
        def _():
            r = t - 2
            for step in range(1, group):
                sender = lax.rem(my_ctx + step, group)
                back_copy(r, sender, sender).wait_recv()
            for k in range(per_round):
                finish(r * per_round + k)

        return carry

    lax.fori_loop(0, rounds + 2, step_body, 0)
    for step in range(1, owners):
        id_copy(step).wait_send()
    for u in range(users):
        for step in range(1, owners):
            row_copy(u, step).wait_send()
    for r in range(rounds):
        for step in range(1, group):
            unit_copy(r, step).wait_send()
            back_copy(r, lax.rem(my_ctx + step, group), my_ctx).wait_send()


def per_device(item_ids, lengths, table, w_in, w_out):
    users, rows = item_ids.shape
    owned, width = table.shape
    owners, group = lax.axis_size("dp"), lax.axis_size("ctx")
    cap = 2 * rows // owners
    size = width // HEADS
    per_round = group // HEADS
    rounds = users // per_round
    total = group * rows
    chunk = math.gcd(owned, 512)
    depth = min(4, owned // chunk)
    back = size + 16
    vmem = pl.BlockSpec(memory_space=pltpu.VMEM)
    hbm = pl.BlockSpec(memory_space=pl.ANY)
    dma = pltpu.SemaphoreType.DMA
    return pl.pallas_call(
        functools.partial(layer_kernel, owners, group),
        out_shape=jax.ShapeDtypeStruct((users, rows, width), BF16),
        in_specs=[pl.BlockSpec(memory_space=pltpu.SMEM), vmem, hbm, hbm, hbm],
        out_specs=vmem,
        scratch_shapes=[
            pltpu.VMEM((owners, users, rows), jnp.int32),
            pltpu.VMEM((users, 1, rows), jnp.int32),
            pltpu.VMEM((owners * users, cap), jnp.int32),
            pltpu.SMEM((owners * users, cap), jnp.int32),
            pltpu.VMEM((depth, chunk, width), BF16),
            pltpu.VMEM((owned, width), F32),
            pltpu.VMEM((cap, width), F32),
            pltpu.VMEM((users, owners, cap, width), BF16),
            pltpu.VMEM((width, 4 * width), BF16),
            pltpu.VMEM((width, width), BF16),
            pltpu.VMEM((users, owners, cap, width), BF16),
            pltpu.VMEM((4 * width, width), BF16),
            pltpu.VMEM((users, rows, width), BF16),
            pltpu.VMEM((users, width, rows), BF16),
            pltpu.VMEM((users, HEADS, 3 * size, rows), BF16),
            pltpu.VMEM((rounds, group, 3 * size, rows), BF16),
            pltpu.VMEM((rounds, group, back, rows), BF16),
            pltpu.VMEM((users, HEADS, back, rows), BF16),
            pltpu.VMEM((total, size), BF16),
            pltpu.VMEM((total, size), BF16),
            pltpu.VMEM((size, total), BF16),
            dma((depth,)),
            dma((2,)),
            dma,
            dma((owners,)),
            dma((owners,)),
            dma((users, owners)),
            dma((users, owners)),
            dma((rounds, group)),
            dma((rounds, group)),
            dma((rounds, group)),
            dma((rounds, group)),
        ],
        compiler_params=pltpu.CompilerParams(
            collective_id=0, has_side_effects=True, vmem_limit_bytes=67_043_328
        ),
    )(lengths, item_ids, table, w_in, w_out)


def solution(mesh):
    return jax.shard_map(
        per_device,
        mesh=mesh,
        in_specs=(P("dp", "ctx"), P("dp"), P("dp", None), P(), P()),
        out_specs=P("dp", "ctx", None),
        check_vma=False,
    )
```

time: 116 us -> 101 us (0.87)
  local copies, waits for them, and re-layouts: 20.7 us -> 2.26 us
  Pallas kernels: 93.3 us -> 98.6 us
    gather x1 -> x0, local copies, waits for them, and re-layouts: 17.2 us -> none  [per_device(): jnp.take(table, index.reshape(-1), axis=0, mode='clip')]
    pallas_call x1, Pallas kernels: 86.6 us -> 98.6 us  [per_device(): pl.pallas_call(functools.partial(layer_kernel, owners, group), out_shape=...]
    pallas_call x1 -> x0, Pallas kernels: 6.68 us -> none  [per_device(): pl.pallas_call(functools.partial(index_kernel, owners, owned, cap), out_s...]
    reshape x1 -> x0, local copies, waits for them, and re-layouts: 1.28 us -> none  [per_device(): item_ids.reshape(users, 1, rows)]
where the time goes in v1:
time: 101 us
  Pallas kernels  98.6 us (98%)
  local copies, waits for them, and re-layouts  2.26 us (2%)
    pallas_call x1, Pallas kernels, per_device(): pl.pallas_call(functools.partial(layer_kernel, owners, group), out_shape=...  98.6 us
    unnamed x1, local copies, waits for them, and re-layouts  2.26 us

profile of v1, /device:TPU:15, one launch (start us, length us, event | category | flops | bytes accessed | tf_op | source)
XLA Modules:
  0.0 100.8 jit_solution(8453471210067833180)
XLA Ops:
  0.0 98.6 %shard_map.55 = bf16[4,256,512]{2,1,0:T(8,128)(2,1)} custom-call(s32[4]{0:T(128)} %lengths_ref.1, s32[4,256]{1,0:T(4,128)} %ids_ref.1, bf16[16384,512]{1,0:T(8,128)(2,1)} %table_ref.1, bf16[512,2048]{1,0:T(8,128)(2,1)} %w_in_ref.1, bf16[512,512]{1,0:T(8,128)(2,1)} %w_out_ref.1), custom_call_target="tpu_custom_call" | custom-call | tf_op jit(solution)/shard_map/pallas_call | solution.py:316
  98.6 2.3 %copy.7 = bf16[4,256,512]{2,1,0:T(8,128)(2,1)} copy(bf16[4,256,512]{2,1,0:T(8,128)(2,1)} %shard_map.55) | data formatting | bytes 2097152

commit v2 on v1

--- a/solution.py
+++ b/solution.py
@@ -308,7 +308,7 @@
     rounds = users // per_round
     total = group * rows
     chunk = math.gcd(owned, 512)
-    depth = min(4, owned // chunk)
+    depth = min(8, owned // chunk)
     back = size + 16
     vmem = pl.BlockSpec(memory_space=pltpu.VMEM)
     hbm = pl.BlockSpec(memory_space=pl.ANY)

time: 101 us -> 97.4 us (0.964)
  Pallas kernels: 98.6 us -> 94.9 us
    pallas_call x1, Pallas kernels: 98.6 us -> 94.9 us  [per_device(): pl.pallas_call(functools.partial(layer_kernel, owners, group), out_shape=...]
where the time goes in v2:
time: 97.4 us; the launch traced here: 97.2 us
  Pallas kernels  94.9 us (97%)
  local copies, waits for them, and re-layouts  2.26 us (2%)
    pallas_call x1, Pallas kernels, per_device(): pl.pallas_call(functools.partial(layer_kernel, owners, group), out_shape=...  94.9 us
    unnamed x1, local copies, waits for them, and re-layouts  2.26 us

profile of v2, /device:TPU:15, one launch (start us, length us, event | category | flops | bytes accessed | tf_op | source)
XLA Modules:
  0.0 97.2 jit_solution(313930323267616248)
XLA Ops:
  0.0 94.9 %shard_map.55 = bf16[4,256,512]{2,1,0:T(8,128)(2,1)} custom-call(s32[4]{0:T(128)} %lengths_ref.1, s32[4,256]{1,0:T(4,128)} %ids_ref.1, bf16[16384,512]{1,0:T(8,128)(2,1)} %table_ref.1, bf16[512,2048]{1,0:T(8,128)(2,1)} %w_in_ref.1, bf16[512,512]{1,0:T(8,128)(2,1)} %w_out_ref.1), custom_call_target="tpu_custom_call" | custom-call | tf_op jit(solution)/shard_map/pallas_call | solution.py:316
  94.9 2.3 %copy.7 = bf16[4,256,512]{2,1,0:T(8,128)(2,1)} copy(bf16[4,256,512]{2,1,0:T(8,128)(2,1)} %shard_map.55) | data formatting | bytes 2097152
